TPU v7x, 32 devices: a whole 2x2x4 slice. The times are simulated.
32 devices in a mesh: ov: 16 (over z, y, core), vec: 2 (over x).
Axes of the slice: x: 2, y: 2, z: 4, core: 2. Of those that a mesh axis runs over, the one named last changes fastest.
Arguments:
- chol_vectors: bfloat16 [196608, 4096], P('ov', 'vec'), may hold values from -3.5 to 3.5
- amplitudes: bfloat16 [196608, 256], P('ov'), may hold values from -0.013671875 to 0.013671875
- sigma_prior: bfloat16 [196608, 256], P(('ov', 'vec')), may hold values from -4 to 4
Outputs:
- sigma_cycle: bfloat16 [196608, 256], P(('ov', 'vec'))
All inputs are finite; a program needn't handle non-finite values.
Results may differ from a plain program's by a relative error of at most 0.0065.
Values may be sent and summed in bfloat16 or wider, within the bound.
A program may use at most 128 MiB of HBM per device.

v0:
```python
import jax
import jax.numpy as jnp
from jax import lax
from jax.sharding import PartitionSpec as P


def body(chol_vectors, amplitudes, sigma_prior):
    contract = (((0,), (0,)), ((), ()))
    partial_x = lax.dot_general(
        chol_vectors, amplitudes, contract, preferred_element_type=jnp.float32
    )
    summed = lax.psum(partial_x, "ov")
    coupling = summed.astype(jnp.bfloat16)
    cycle = lax.psum_scatter(
        jnp.dot(chol_vectors, coupling, preferred_element_type=jnp.float32),
        "vec",
        scatter_dimension=0,
        tiled=True,
    )
    return (sigma_prior.astype(jnp.float32) + cycle).astype(jnp.bfloat16)


def solution(mesh):
    return jax.shard_map(
        body,
        mesh=mesh,
        in_specs=(P("ov", "vec"), P("ov", None), P(("ov", "vec"), None)),
        out_specs=P(("ov", "vec"), None),
        check_vma=False,
    )
```

profile of v0, /device:TPU:0, one launch (start us, length us, event | category | flops | bytes accessed | tf_op | source)
XLA Modules:
  0.0 287.8 jit_solution(18080904443797007626)
XLA Ops:
  6.5 0.0 reduce-scatter.2.cloned.1.call-start
  6.5 21.7 %fusion.1 = f32[2048,256]{1,0:T(8,128)S(1)} fusion(bf16[12288,2048]{1,0:T(8,128)(2,1)} %param.3, bf16[12288,256]{1,0:T(8,128)(2,1)} %param.4), kind=kOutput, calls=%fused_computation.3 | convolution fusion | flops 12884901888 | bytes 58720256 | tf_op jit(solution)/shard_map/dot_general | solution.py:9
  28.3 76.9 %all-reduce.1 = bf16[2048,256]{1,0:T(8,128)(2,1)S(1)} all-reduce(f32[2048,256]{1,0:T(8,128)S(1)} %fusion.1), channel_id=1, replica_groups=mesh['ov'=16,'vec'=2] {'ov'}, use_global_device_ids=true, to_apply=%region_0.0 | all-reduce | flops 524288 | bytes 3145728 | tf_op jit(solution)/shard_map/psum | solution.py:12
  105.1 23.9 %convolution_bitcast_fusion = f32[12288,256]{0,1:T(8,128)} fusion(bf16[12288,2048]{1,0:T(8,128)(2,1)} %param.3, bf16[2048,256]{1,0:T(8,128)(2,1)S(1)} %all-reduce.1), kind=kOutput, calls=%fused_computation | convolution fusion | flops 12884901888 | bytes 63963136 | tf_op jit(solution)/shard_map/dot_general | solution.py:15
  129.1 0.0 reduce-scatter.2.cloned.1.call-update
  129.1 3.2 %copy.4 = bf16[6144,256]{0,1:T(8,128)(2,1)S(1)} copy(bf16[6144,256]{1,0:T(8,128)(2,1)} %param.5) | data formatting | bytes 6291456 | tf_op args[2]
  132.3 138.7 %reduce-scatter.2.cloned.1.call-done = f32[6144,256]{0,1:T(8,128)} async-done(((f32[12288,256]{0,1:T(8,128)}), f32[6144,256]{0,1:T(8,128)}) %reduce-scatter.2.cloned.1.call-update) | async-done | bytes 6291472 | tf_op jit(solution)/shard_map/reduce_scatter | solution.py:14
  271.0 5.3 %add_convert_fusion = bf16[6144,256]{0,1:T(8,128)(2,1)} fusion(f32[6144,256]{0,1:T(8,128)} %reduce-scatter.2.cloned.1.call-done, bf16[6144,256]{0,1:T(8,128)(2,1)S(1)} %copy.4), kind=kLoop, calls=%fused_computation.1 | loop fusion | flops 4718592 | bytes 12582912 | tf_op jit(solution)/shard_map/convert_element_type | solution.py:20
  276.3 4.6 %copy.5 = bf16[6144,256]{1,0:T(8,128)(2,1)} copy(bf16[6144,256]{0,1:T(8,128)(2,1)} %add_convert_fusion) | data formatting | bytes 6291456 | tf_op jit(solution)/shard_map/convert_element_type | solution.py:20
Async XLA Ops:
  6.5 264.5 %reduce-scatter.2.cloned.1.call-start = ((), (), s32[]{:S(2)}) async-start(), calls=%async_computation.1 | async-start | bytes 18874368 | tf_op jit(solution)/shard_map/reduce_scatter | solution.py:14
Sparse Core Ops, SparseCore 0:
  129.2 141.7 reduce-scatter.1
where the time goes:
time: 288 us
  waiting for transfers between devices  139 us (48%)
  blocking collectives  76.9 us (27%)
  matrix products  45.6 us (16%)
  between operations  13.4 us (5%)
  local copies, waits for them, and re-layouts  7.82 us (3%)
  other arithmetic  5.28 us (2%)
    reduce_scatter x1, waiting for transfers between devices, body(): lax.psum_scatter(jnp.dot(chol_vectors, coupling, preferred_element_type=j...  139 us
    psum x1, blocking collectives, body(): summed = lax.psum(partial_x, 'ov')  76.9 us
    dot_general x1, matrix products, body(): jnp.dot(chol_vectors, coupling, preferred_element_type=jnp.float32)  23.9 us
    dot_general x1, matrix products, body(): lax.dot_general(chol_vectors, amplitudes, contract, preferred_element_typ...  21.7 us
  transfers between devices with their start and end apart: 1, of which 1 were waited for; matrix products, arithmetic and copies ran while one was open for 1% of the time, Pallas kernels for 0%

commit v1 on v0

--- a/solution.py
+++ b/solution.py
@@ -5,11 +5,17 @@
 
 
 def body(chol_vectors, amplitudes, sigma_prior):
+
+    def link_notes(target):
+        z_new = jax.lax.all_gather(target, "ov")
+        local_next = jnp.sum(z_new, axis=0)
+        return local_next
+
     contract = (((0,), (0,)), ((), ()))
     partial_x = lax.dot_general(
         chol_vectors, amplitudes, contract, preferred_element_type=jnp.float32
     )
-    summed = lax.psum(partial_x, "ov")
+    summed = link_notes(partial_x)
     coupling = summed.astype(jnp.bfloat16)
     cycle = lax.psum_scatter(
         jnp.dot(chol_vectors, coupling, preferred_element_type=jnp.float32),

time: 288 us -> 400 us (1.39)
  waiting for transfers between devices: 139 us -> 312 us
  blocking collectives: 76.9 us -> 0 us
  other arithmetic: 5.28 us -> 17.4 us
    all_gather x0 -> x1, waiting for transfers between devices: none -> 171 us  [link_notes(): z_new = jax.lax.all_gather(target, 'ov')]
    psum x1 -> x0, blocking collectives: 76.9 us -> none  [body(): summed = lax.psum(partial_x, 'ov')]
    reduce_sum x0 -> x1, other arithmetic: none -> 12.2 us  [link_notes(): local_next = jnp.sum(z_new, axis=0)]
  transfers between devices with their start and end apart: 1 -> 2, of which waited for: 1 -> 2; matrix products, arithmetic and copies ran while one was open for 1% -> 1% of each run, Pallas kernels for 0% -> 0%
where the time goes in v1:
time: 400 us; the launch traced here: 399 us
  waiting for transfers between devices  312 us (78%)
  matrix products  48.1 us (12%)
  other arithmetic  17.4 us (4%)
  between operations  13.4 us (3%)
  local copies, waits for them, and re-layouts  7.82 us (2%)
    all_gather x1, waiting for transfers between devices, link_notes(): z_new = jax.lax.all_gather(target, 'ov')  171 us
    reduce_scatter x1, waiting for transfers between devices, body(): lax.psum_scatter(jnp.dot(chol_vectors, coupling, preferred_element_type=j...  141 us
    dot_general x1, matrix products, body(): lax.dot_general(chol_vectors, amplitudes, contract, preferred_element_typ...  24.1 us
    dot_general x1, matrix products, body(): jnp.dot(chol_vectors, coupling, preferred_element_type=jnp.float32)  24 us
    reduce_sum x1, other arithmetic, link_notes(): local_next = jnp.sum(z_new, axis=0)  12.2 us
  transfers between devices with their start and end apart: 2, of which 2 were waited for; matrix products, arithmetic and copies ran while one was open for 1% of the time, Pallas kernels for 0%

profile of v1, /device:TPU:0, one launch (start us, length us, event | category | flops | bytes accessed | tf_op | source)
XLA Modules:
  0.0 399.1 jit_solution(9852529187954831884)
XLA Ops:
  6.5 0.0 all-gather.3.cloned.1.call-start
  6.5 24.1 %fusion.1 = f32[2048,256]{1,0:T(8,128)} fusion(bf16[12288,2048]{1,0:T(8,128)(2,1)} %param.3, bf16[12288,256]{1,0:T(8,128)(2,1)} %param.4), kind=kOutput, calls=%fused_computation.3 | convolution fusion | flops 12884901888 | bytes 58720256 | tf_op jit(solution)/shard_map/dot_general | solution.py:15
  30.6 0.0 all-gather.3.cloned.1.call-update
  30.6 0.0 reduce-scatter.2.cloned.1.call-start
  30.7 170.9 %all-gather.3.cloned.1.call-done = f32[32768,256]{1,0:T(8,128)} async-done(((f32[2048,256]{1,0:T(8,128)}), f32[32768,256]{1,0:T(8,128)}) %all-gather.3.cloned.1.call-update) | async-done | bytes 33554448 | tf_op jit(solution)/shard_map/all_gather | solution.py:10
  201.5 12.2 %reduce_sum.9 = bf16[2048,256]{1,0:T(8,128)(2,1)S(1)} reduce(f32[16,2048,256]{2,1,0:T(8,128)} %bitcast.7, f32[]{:T(128)} %constant.0.clone.1), dimensions={0}, to_apply=%region_0.0 | reduce | flops 7864320 | bytes 34603012 | tf_op jit(solution)/shard_map/reduce_sum | solution.py:11
  213.7 24.0 %convolution_bitcast_fusion = f32[12288,256]{0,1:T(8,128)} fusion(bf16[12288,2048]{1,0:T(8,128)(2,1)} %param.3, bf16[2048,256]{1,0:T(8,128)(2,1)S(1)} %reduce_sum.9), kind=kOutput, calls=%fused_computation | convolution fusion | flops 12884901888 | bytes 63963136 | tf_op jit(solution)/shard_map/dot_general | solution.py:21
  237.7 0.0 reduce-scatter.2.cloned.1.call-update
  237.7 3.2 copy.4
  240.9 141.5 %reduce-scatter.2.cloned.1.call-done = f32[6144,256]{0,1:T(8,128)} async-done(((f32[12288,256]{0,1:T(8,128)}), f32[6144,256]{0,1:T(8,128)}) %reduce-scatter.2.cloned.1.call-update) | async-done | bytes 6291472 | tf_op jit(solution)/shard_map/reduce_scatter | solution.py:20
  382.4 5.3 %add_convert_fusion = bf16[6144,256]{0,1:T(8,128)(2,1)} fusion(f32[6144,256]{0,1:T(8,128)} %reduce-scatter.2.cloned.1.call-done, bf16[6144,256]{0,1:T(8,128)(2,1)S(1)} %copy.4), kind=kLoop, calls=%fused_computation.1 | loop fusion | flops 4718592 | bytes 12582912 | tf_op jit(solution)/shard_map/convert_element_type | solution.py:26
  387.7 4.6 %copy.5 = bf16[6144,256]{1,0:T(8,128)(2,1)} copy(bf16[6144,256]{0,1:T(8,128)(2,1)} %add_convert_fusion) | data formatting | bytes 6291456 | tf_op jit(solution)/shard_map/convert_element_type | solution.py:26
Async XLA Ops:
  6.5 195.0 %all-gather.3.cloned.1.call-start = ((), (), s32[]{:S(2)}) async-start(), calls=%async_computation.2 | async-start | bytes 35651584 | tf_op jit(solution)/shard_map/all_gather | solution.py:10
  30.6 351.8 %reduce-scatter.2.cloned.1.call-start = ((), (), s32[]{:S(2)}) async-start(), calls=%async_computation.1 | async-start | bytes 18874368 | tf_op jit(solution)/shard_map/reduce_scatter | solution.py:20
Sparse Core Ops, SparseCore 0:
  30.7 170.7 all-gather.2
  237.8 144.5 reduce-scatter.1
